TPU v7x, 32 devices: a whole 2x2x4 slice. The times are simulated.
32 devices in a mesh: elem: 16 (over z, y, core), band: 2 (over x).
Axes of the slice: x: 2, y: 2, z: 4, core: 2. Of those that a mesh axis runs over, the one named last changes fastest.
Arguments:
- y_current: bfloat16 [512, 64, 512], P('elem', None, 'band'), may hold values from -6 to 6
- y_previous: bfloat16 [512, 64, 512], P('elem', None, 'band'), may hold values from -6 to 6
- h_blocks: bfloat16 [512, 64, 320], P('elem'), may hold values from -0.3125 to 0.3125
- basis_sizes: int32 [512], P('elem'), may hold values from 40 to 64
- neighbours: int32 [512, 4], P('elem'), may hold values from 0 to 511, as said below
Outputs:
- filtered: bfloat16 [512, 64, 512], P('elem', None, 'band')
- margin: float32 [512, 512], P('elem', 'band')
Inputs may be any that keep to these rules, and one draw needn't show every extreme that they name: `neighbours`: the elements lie on a periodic grid of 32 x 16; row i lists the elements that share an edge with element i, in the order previous grid row, next grid row, previous column, next column, so adjacency is symmetric. Element g belongs to index g // 32 of elem, whose elements fill 2 consecutive grid rows in some order; a neighbour therefore belongs to the same index or to one of the two beside it, periodically, and exactly 16 of an index's elements have a neighbour on the next index, and 16 on the previous one.
All inputs are finite; a program needn't handle non-finite values.
Results may differ from a plain program's by a relative error of at most 0.018.
Values may be sent and summed in bfloat16 or wider, within the bound.
A program may use at most 64 MiB of HBM per device.

v0:
```python
import jax
import jax.numpy as jnp
from jax import lax
from jax.sharding import PartitionSpec as P

BMAX = 64
GY = 16
DEGREES = 2


center_value = 0.3
spectral_half = 1.7


def shifted(block, axis, distance):
    devices = range(lax.axis_size(axis))
    route = [((i - distance) % len(devices), i) for i in devices]
    return lax.ppermute(block, axis, route)


def referenced_slots(relative, local_index, wanted, local_count):
    positions = jnp.arange(local_count, dtype=jnp.int32)
    marked = jnp.where(relative == wanted, local_index, -1)
    present = jnp.any(marked[:, :, None] == positions[None, None, :], axis=(0, 1))
    return jnp.cumsum(present.astype(jnp.int32)) - 1


def on_device(y_current, y_previous, h_blocks, basis_sizes, neighbours):
    local_count = neighbours.shape[0]
    band_width = y_current.shape[2]
    count_elem = lax.axis_size("elem")
    myself = lax.axis_index("elem")
    owners = neighbours // local_count
    local_index = neighbours % local_count
    relative = (owners - myself + 1) % count_elem - 1
    send_next = jnp.nonzero(jnp.any(relative == 1, axis=1), size=GY)[0]
    send_prev = jnp.nonzero(jnp.any(relative == -1, axis=1), size=GY)[0]
    slot_prev = referenced_slots(relative, local_index, -1, local_count)
    slot_next = referenced_slots(relative, local_index, 1, local_count)
    pool_index = jnp.where(
        relative == 0,
        local_index,
        jnp.where(
            relative == -1,
            local_count + jnp.take(slot_prev, local_index),
            local_count + GY + jnp.take(slot_next, local_index),
        ),
    )
    row_mask = (jnp.arange(BMAX, dtype=jnp.int32)[None, :] < basis_sizes[:, None]).astype(
        jnp.bfloat16
    )[:, :, None]
    mask_float = row_mask.astype(jnp.float32)
    current = y_current * row_mask
    previous = y_previous * row_mask
    for degree in range(DEGREES):
        from_prev = shifted(current[send_next], "elem", 1)
        from_next = shifted(current[send_prev], "elem", -1)
        pool = jnp.concatenate([current, from_prev, from_next], axis=0)
        nearby = pool[pool_index]
        stacked = jnp.concatenate([current[:, None], nearby], axis=1).reshape(
            local_count, 5 * BMAX, band_width
        )
        applied = jnp.einsum("irc,icb->irb", h_blocks, stacked, preferred_element_type=jnp.float32)
        following = mask_float * (
            2.0 / spectral_half * (applied - center_value * current.astype(jnp.float32))
            - previous.astype(jnp.float32)
        )
        previous = current
        current = following.astype(jnp.bfloat16)
    flat = current.reshape(local_count * BMAX, band_width)
    gathered = lax.all_gather(flat, "band", axis=1, tiled=True)
    summed = lax.psum_scatter(
        lax.dot_general(
            gathered, flat, (((0,), (0,)), ((), ())), preferred_element_type=jnp.float32
        ).astype(jnp.bfloat16),
        "elem",
        scatter_dimension=0,
        tiled=True,
    ).astype(jnp.float32)
    margin = summed / jnp.float32(local_count * count_elem * BMAX)
    return (current, margin)


def solution(mesh):
    in_specs = (
        P("elem", None, "band"),
        P("elem", None, "band"),
        P("elem", None, None),
        P("elem"),
        P("elem", None),
    )
    out_specs = (P("elem", None, "band"), P("elem", "band"))
    return jax.shard_map(
        on_device, mesh=mesh, in_specs=in_specs, out_specs=out_specs, check_vma=False
    )
```

profile of v0, /device:TPU:0, one launch (start us, length us, event | category | flops | bytes accessed | tf_op | source)
XLA Modules:
  0.0 174.4 jit_solution(13674862233385489575)
XLA Ops:
  7.2 0.0 copy-start
  7.2 0.0 all-gather.2.cloned.1.call-start
  7.2 0.9 copy.31
  8.2 0.1 reduce_or.36
  8.3 0.6 convert_reduce_fusion.1
  8.9 0.7 fusion.27
  9.6 0.1 copy.35
  9.7 0.1 reduce-window.30
  9.8 0.1 fusion.14
  9.9 0.8 scatter_custom_fusion
  10.7 0.1 copy.36
  10.8 0.8 fusion.25
  11.6 1.6 broadcast_multiply_fusion
  13.1 0.6 gather_fusion
  13.7 0.5 collective-permute-start
  14.3 0.1 fusion.32
  14.4 0.6 convert_reduce_fusion
  15.0 0.1 copy.37
  15.1 0.1 reduce-window.31
  15.2 0.1 fusion.15
  15.3 0.8 scatter_custom_fusion.1
  16.1 0.1 copy.38
  16.2 0.8 fusion.26
  17.0 1.4 gather_fusion.1
  18.4 5.0 %collective-permute-start.1 = (bf16[16,64,256]{2,1,0:T(8,128)(2,1)}, bf16[16,64,256]{2,1,0:T(8,128)(2,1)}, u32[]{:S(2)}, u32[]{:S(2)}) collective-permute-start(bf16[16,64,256]{2,1,0:T(8,128)(2,1)} %gather_fusion.1), channel_id=1, source_target_pairs={{2,0},{4,2},{6,4},{8,6},{10,8},{12,10},{14,12},{16,14},{18,16},{20... | collective-permute-start | bytes 1572872 | tf_op jit(solution)/shard_map/ppermute | solution.py:18
  23.4 0.1 copy.39
  23.4 0.1 fusion.8
  23.6 0.1 copy.40
  23.6 0.1 reduce-window.32
  23.7 0.1 add_reduce_fusion.1
  23.8 0.1 copy.41
  23.9 0.1 fusion.9
  24.0 0.1 reshape.406
  24.1 1.2 gather_fusion.6
  25.4 0.1 reshape.409
  25.5 0.1 copy.42
  25.6 0.1 reduce-window.33
  25.6 0.1 add_reduce_fusion
  25.7 1.2 gather_fusion.7
  27.0 0.1 reshape.413
  27.1 0.1 reshape.352
  27.2 2.5 %fusion.40 = bf16[32,1,64,256]{3,2,1,0:T(8,128)(2,1)} fusion(bf16[32,64,256]{2,1,0:T(8,128)(2,1)} %param.7, bf16[32,64]{1,0:T(8,128)(2,1)S(1)} %get-tuple-element.9), kind=kLoop, calls=%fused_computation.97 | loop fusion | flops 524288 | bytes 2101248 | tf_op jit(solution)/shard_map/broadcast_in_dim | solution.py:60
  29.8 0.0 collective-permute-done
  29.8 0.6 collective-permute-done.1
  30.4 2.8 %pad_maximum_fusion.2 = bf16[64,64,256]{2,1,0:T(8,128)(2,1)} fusion(bf16[16,64,256]{2,1,0:T(8,128)(2,1)} %collective-permute-done.1, bf16[16,64,256]{2,1,0:T(8,128)(2,1)} %collective-permute-done, bf16[32,64,256]{2,1,0:T(8,128)(2,1)S(1)} %broadcast_multiply_fusion), kind=kLoop, calls=%fused_computation.21 | loop fusion | flops 2097152 | bytes 4194304 | tf_op jit(solution)/shard_map/concatenate | solution.py:58
  33.1 4.3 %gather_fusion.2 = bf16[128,64,256]{2,1,0:T(8,128)(2,1)} fusion(bf16[64,64,256]{2,1,0:T(8,128)(2,1)} %pad_maximum_fusion.2, s32[1024]{0:T(1024)S(1)} %pad_clamp_fusion), kind=kCustom, calls=%fused_computation.4 | custom fusion | bytes 8389120 | tf_op jit(solution)/shard_map/gather | solution.py:59
  37.5 3.0 %pad_maximum_fusion = bf16[32,5,64,256]{3,2,1,0:T(8,128)(2,1)S(1)} fusion(bf16[32,4,64,256]{3,2,1,0:T(8,128)(2,1)} %bitcast.39, bf16[32,1,64,256]{3,2,1,0:T(8,128)(2,1)} %fusion.40), kind=kLoop, calls=%fused_computation.10 | loop fusion | flops 2621440 | bytes 10485760 | tf_op jit(solution)/shard_map/concatenate | solution.py:60
  40.5 2.3 %fusion.4 = bf16[32,64,256]{2,1,0:T(8,128)(2,1)} fusion(bf16[32,64,256]{2,1,0:T(8,128)(2,1)S(1)} %broadcast_multiply_fusion, bf16[32,64,320]{2,1,0:T(8,128)(2,1)S(1)} %copy-done, bf16[32,320,256]{2,1,0:T(8,128)(2,1)S(1)} %bitcast.37, bf16[32,64,256]{2,1,0:T(8,128)(2,1)S(1)} %copy-done.2, f32[32,64]{1,0:T(8,128)S(1)} %get-tuple-element.8, ...), kind=kOutput, calls=%fused_computation.18 | convolution fusion | flops 340262912 | bytes 9711616 | tf_op jit(solution)/shard_map/irc,icb->irb/dot_general | solution.py:63
  42.9 1.8 %gather_fusion.4 = bf16[16,64,256]{2,1,0:T(8,128)(2,1)S(1)} fusion(bf16[32,64,256]{2,1,0:T(8,128)(2,1)} %fusion.4, s32[1024]{0:T(1024)S(1)} %pad_clamp_fusion.2), kind=kCustom, calls=%fused_computation.6 | custom fusion | bytes 1048640 | tf_op jit(solution)/shard_map/gather | solution.py:57
  44.7 2.6 %gather_fusion.3 = bf16[16,64,256]{2,1,0:T(8,128)(2,1)} fusion(bf16[32,64,256]{2,1,0:T(8,128)(2,1)} %fusion.4, s32[1024]{0:T(1024)S(1)} %pad_clamp_fusion.3), kind=kCustom, calls=%fused_computation.5 | custom fusion | bytes 1048640 | tf_op jit(solution)/shard_map/gather | solution.py:56
  47.3 1.3 collective-permute-start.2
  48.6 3.3 %collective-permute-start.3 = (bf16[16,64,256]{2,1,0:T(8,128)(2,1)S(1)}, bf16[16,64,256]{2,1,0:T(8,128)(2,1)S(1)}, u32[]{:S(2)}, u32[]{:S(2)}) collective-permute-start(bf16[16,64,256]{2,1,0:T(8,128)(2,1)S(1)} %gather_fusion.4), channel_id=1, source_target_pairs={{2,0},{4,2},{6,4},{8,6},{10,8},{12,10},{14,12},{16,14},{18,16},{20... | collective-permute-start | bytes 1572872 | tf_op jit(solution)/shard_map/ppermute | solution.py:18
  51.9 7.2 %collective-permute-done.2 = bf16[16,64,256]{2,1,0:T(8,128)(2,1)S(1)} collective-permute-done((bf16[16,64,256]{2,1,0:T(8,128)(2,1)}, bf16[16,64,256]{2,1,0:T(8,128)(2,1)S(1)}, u32[]{:S(2)}, u32[]{:S(2)}) %collective-permute-start.2) | collective-permute-done | bytes 524320 | tf_op jit(solution)/shard_map/ppermute | solution.py:18
  59.1 2.8 %pad_maximum_fusion.3 = bf16[64,64,256]{2,1,0:T(8,128)(2,1)} fusion(bf16[16,64,256]{2,1,0:T(8,128)(2,1)S(1)} %collective-permute-done.3, bf16[16,64,256]{2,1,0:T(8,128)(2,1)S(1)} %collective-permute-done.2, bf16[32,64,256]{2,1,0:T(8,128)(2,1)} %fusion.4), kind=kLoop, calls=%fused_computation.22 | loop fusion | flops 2097152 | bytes 4194304 | tf_op jit(solution)/shard_map/concatenate | solution.py:58
  61.8 4.3 %gather_fusion.5 = bf16[128,64,256]{2,1,0:T(8,128)(2,1)} fusion(bf16[64,64,256]{2,1,0:T(8,128)(2,1)} %pad_maximum_fusion.3, s32[1024]{0:T(1024)S(1)} %pad_clamp_fusion), kind=kCustom, calls=%fused_computation.7 | custom fusion | bytes 8389120 | tf_op jit(solution)/shard_map/gather | solution.py:59
  66.2 3.0 %pad_maximum_fusion.1 = bf16[32,5,64,256]{3,2,1,0:T(8,128)(2,1)S(1)} fusion(bf16[32,4,64,256]{3,2,1,0:T(8,128)(2,1)} %bitcast.40, bf16[32,1,64,256]{3,2,1,0:T(8,128)(2,1)} %bitcast.36), kind=kLoop, calls=%fused_computation.11 | loop fusion | flops 2621440 | bytes 10485760 | tf_op jit(solution)/shard_map/concatenate | solution.py:60
  69.2 2.3 %fusion.6 = bf16[32,64,256]{2,1,0:T(8,128)(2,1)} fusion(bf16[32,64,256]{2,1,0:T(8,128)(2,1)S(1)} %broadcast_multiply_fusion, bf16[32,64,256]{2,1,0:T(8,128)(2,1)S(1)} %copy-done.1, bf16[32,64,320]{2,1,0:T(8,128)(2,1)S(1)} %copy-done, bf16[32,320,256]{2,1,0:T(8,128)(2,1)S(1)} %bitcast.38, f32[32,64]{1,0:T(8,128)S(1)} %get-tuple-element.8), kind=kOutput, calls=%fused_computation.20 | convolution fusion | flops 339738624 | bytes 9707520 | tf_op jit(solution)/shard_map/irc,icb->irb/dot_general | solution.py:63
  71.5 0.0 all-gather.2.cloned.1.call-update
  71.5 0.0 reduce-scatter.2.cloned.1.call-start
  71.6 35.4 %all-gather.2.cloned.1.call-done = bf16[2048,512]{1,0:T(8,128)(2,1)} async-done(((bf16[2048,256]{1,0:T(8,128)(2,1)}), bf16[2048,512]{1,0:T(8,128)(2,1)}) %all-gather.2.cloned.1.call-update) | async-done | bytes 2097168 | tf_op jit(solution)/shard_map/all_gather | solution.py:71
  107.0 3.3 %convolution_convert_fusion = bf16[512,256]{1,0:T(8,128)(2,1)} fusion(bf16[2048,512]{1,0:T(8,128)(2,1)} %all-gather.2.cloned.1.call-done, bf16[2048,256]{1,0:T(8,128)(2,1)} %bitcast.42), kind=kOutput, calls=%fused_computation.25 | convolution fusion | flops 537001984 | bytes 3407872 | tf_op jit(solution)/shard_map/dot_general | solution.py:73
  110.3 0.0 reduce-scatter.2.cloned.1.call-update
  110.3 55.9 %reduce-scatter.2.cloned.1.call-done = bf16[32,256]{1,0:T(8,128)(2,1)} async-done(((bf16[512,256]{1,0:T(8,128)(2,1)}), bf16[32,256]{1,0:T(8,128)(2,1)}) %reduce-scatter.2.cloned.1.call-update) | async-done | bytes 16400 | tf_op jit(solution)/shard_map/reduce_scatter | solution.py:72
  166.2 1.3 convert_multiply_fusion.1
  (20 shorter events, 0.2 us)
Async XLA Ops:
  7.2 33.3 %copy-start = (bf16[32,64,320]{2,1,0:T(8,128)(2,1)S(1)}, bf16[32,64,320]{2,1,0:T(8,128)(2,1)}, u32[]{:S(2)}) copy-start(bf16[32,64,320]{2,1,0:T(8,128)(2,1)} %param.9) | copy-start | bytes 3932164
  7.2 99.8 %all-gather.2.cloned.1.call-start = ((), (), s32[]{:S(2)}) async-start(), calls=%async_computation.1 | async-start | bytes 3145728 | tf_op jit(solution)/shard_map/all_gather | solution.py:71
  13.7 16.0 %collective-permute-start = (bf16[16,64,256]{2,1,0:T(8,128)(2,1)S(1)}, bf16[16,64,256]{2,1,0:T(8,128)(2,1)}, u32[]{:S(2)}, u32[]{:S(2)}) collective-permute-start(bf16[16,64,256]{2,1,0:T(8,128)(2,1)S(1)} %gather_fusion), channel_id=1, source_target_pairs={{30,0},{0,2},{2,4},{4,6},{6,8},{8,10},{10,12},{12,14},{14,16},{16,... | collective-permute-start | bytes 1572872 | tf_op jit(solution)/shard_map/ppermute | solution.py:18
  18.4 12.0 %collective-permute-start.1 = (bf16[16,64,256]{2,1,0:T(8,128)(2,1)}, bf16[16,64,256]{2,1,0:T(8,128)(2,1)}, u32[]{:S(2)}, u32[]{:S(2)}) collective-permute-start(bf16[16,64,256]{2,1,0:T(8,128)(2,1)} %gather_fusion.1), channel_id=1, source_target_pairs={{2,0},{4,2},{6,4},{8,6},{10,8},{12,10},{14,12},{16,14},{18,16},{20... | collective-permute-start | bytes 1572872 | tf_op jit(solution)/shard_map/ppermute | solution.py:18
  37.5 3.0 %copy-start.2 = (bf16[32,64,256]{2,1,0:T(8,128)(2,1)S(1)}, bf16[32,64,256]{2,1,0:T(8,128)(2,1)}, u32[]{:S(2)}) copy-start(bf16[32,64,256]{2,1,0:T(8,128)(2,1)} %param.8) | copy-start | bytes 3145732
  47.3 11.8 %collective-permute-start.2 = (bf16[16,64,256]{2,1,0:T(8,128)(2,1)}, bf16[16,64,256]{2,1,0:T(8,128)(2,1)S(1)}, u32[]{:S(2)}, u32[]{:S(2)}) collective-permute-start(bf16[16,64,256]{2,1,0:T(8,128)(2,1)} %gather_fusion.3), channel_id=1, source_target_pairs={{30,0},{0,2},{2,4},{4,6},{6,8},{8,10},{10,12},{12,14},{14,16},{16,... | collective-permute-start | bytes 1572872 | tf_op jit(solution)/shard_map/ppermute | solution.py:18
  48.6 10.5 %collective-permute-start.3 = (bf16[16,64,256]{2,1,0:T(8,128)(2,1)S(1)}, bf16[16,64,256]{2,1,0:T(8,128)(2,1)S(1)}, u32[]{:S(2)}, u32[]{:S(2)}) collective-permute-start(bf16[16,64,256]{2,1,0:T(8,128)(2,1)S(1)} %gather_fusion.4), channel_id=1, source_target_pairs={{2,0},{4,2},{6,4},{8,6},{10,8},{12,10},{14,12},{16,14},{18,16},{20... | collective-permute-start | bytes 1572872 | tf_op jit(solution)/shard_map/ppermute | solution.py:18
  66.2 3.0 %copy-start.1 = (bf16[32,64,256]{2,1,0:T(8,128)(2,1)S(1)}, bf16[32,64,256]{2,1,0:T(8,128)(2,1)}, u32[]{:S(2)}) copy-start(bf16[32,64,256]{2,1,0:T(8,128)(2,1)} %fusion.4) | copy-start | bytes 3145732
  71.5 94.7 %reduce-scatter.2.cloned.1.call-start = ((), (), s32[]{:S(2)}) async-start(), calls=%async_computation.2 | async-start | bytes 278528 | tf_op jit(solution)/shard_map/reduce_scatter | solution.py:72
Sparse Core Ops, SparseCore 0:
  71.7 35.2 all-gather.1
  110.5 55.7 reduce-scatter.1
where the time goes:
time: 175 us; the launch traced here: 174 us
  waiting for transfers between devices  99.1 us (57%)
  other arithmetic  23.4 us (13%)
  local copies, waits for them, and re-layouts  19.5 us (11%)
  between operations  14.2 us (8%)
  starting transfers between devices  10.2 us (6%)
  matrix products  7.97 us (5%)
    reduce_scatter x1, waiting for transfers between devices, on_device(): lax.psum_scatter(lax.dot_general(gathered, flat, (((0,), (0,)), ((), ()))...  55.9 us
    all_gather x1, waiting for transfers between devices, on_device(): gathered = lax.all_gather(flat, 'band', axis=1, tiled=True)  35.4 us
    ppermute x4, starting transfers between devices, shifted(): return lax.ppermute(block, axis, route)  10.2 us
    gather x2, local copies, waits for them, and re-layouts, on_device(): nearby = pool[pool_index]  8.66 us
    ppermute x4, waiting for transfers between devices, shifted(): return lax.ppermute(block, axis, route)  7.79 us
    concatenate x2, other arithmetic, on_device(): jnp.concatenate([current[:, None], nearby], axis=1)  6.05 us
    concatenate x2, other arithmetic, on_device(): pool = jnp.concatenate([current, from_prev, from_next], axis=0)  5.56 us
    dot_general x2, matrix products, on_device(): jnp.einsum('irc,icb->irb', h_blocks, stacked, preferred_element_type=jnp....  4.64 us
  transfers between devices with their start and end apart: 6, of which 4 were waited for; matrix products, arithmetic and copies ran while one was open for 6% of the time, Pallas kernels for 0%

commit v1 on v0

v1 whole, which is shorter than its diff:
```python
import functools

import jax
import jax.numpy as jnp
from jax import lax
from jax.experimental import pallas as pl
from jax.experimental.pallas import tpu as pltpu
from jax.sharding import PartitionSpec as P

CHUNKS = 4
center_value = 0.3
spectral_half = 1.7
MESH = pl.DeviceIdType.MESH
ROWS = (((0,), (0,)), ((), ()))


def kernel(
    count_elem, count_band,
    pos_ref, perm_ref, neigh_ref, size_ref, cur_hbm, prev_hbm, h_hbm,
    out_hbm, margin_ref,
    cur, prev, h, y1, y2, f, ordered, halo, other, gram, cross,
    w, v, w1, v1, w2, v2, rw, rv,
    load_sem, out_sem, halo_send, halo_recv, x_send, x_recv,
    pair_send, pair_recv, w_send, w_recv, v_send, v_recv,
):
    e = lax.axis_index("elem")
    b = lax.axis_index("band")
    local, bmax, bands = y1.shape
    edge = local // 2
    q = edge // CHUNKS
    half = count_elem // 2
    rows = margin_ref.shape[0]
    per_block = bands // rows
    after = lax.rem(e + 1, count_elem)
    before = lax.rem(e + count_elem - 1, count_elem)
    parity = lax.rem(e, 2)
    pair = lax.div(e, 2)
    partner = e + 1 - 2 * parity

    loads = [
        pltpu.make_async_copy(src, dst, load_sem.at[k])
        for k, (src, dst) in enumerate(((cur_hbm, cur), (prev_hbm, prev), (h_hbm, h)))
    ]
    for load in loads:
        load.start()

    barrier = pltpu.get_barrier_semaphore()
    for target in (after, before):
        pl.semaphore_signal(barrier, inc=1, device_id=(target, b), device_id_type=MESH)
    for j in range(count_band):
        for d in range(half):
            if j or d:
                target = (2 * lax.rem(pair + d, half) + parity, lax.rem(b + j, count_band))
                pl.semaphore_signal(barrier, inc=1, device_id=target, device_id_type=MESH)

    row_index = lax.broadcasted_iota(jnp.int32, (bmax, bands), 0)

    loads[0].wait()

    def place(p, _):
        i = perm_ref[p]
        y1[p] = jnp.where(row_index < size_ref[i], cur[i].astype(jnp.float32), 0.0).astype(jnp.bfloat16)
        return 0

    lax.fori_loop(0, local, place, 0, unroll=4)
    pl.semaphore_wait(barrier, 2 + half * count_band - 1)

    def halo_copy(degree, side, c, source):
        return pltpu.make_async_remote_copy(
            src_ref=source.at[pl.ds(side * edge + c * q, q)],
            dst_ref=halo.at[degree, 1 - side, pl.ds(c * q, q)],
            send_sem=halo_send.at[degree, side, c],
            recv_sem=halo_recv.at[degree, 1 - side, c],
            device_id=(after if side else before, b),
            device_id_type=MESH,
        )

    def halo_arrived(degree, side, c):
        pltpu.make_async_remote_copy(
            src_ref=y1.at[pl.ds(0, q)],
            dst_ref=halo.at[degree, side, pl.ds(c * q, q)],
            send_sem=halo_send.at[degree, side, c],
            recv_sem=halo_recv.at[degree, side, c],
            device_id=(after if side else before, b),
            device_id_type=MESH,
        ).wait_recv()

    for c in range(CHUNKS):
        for side in (0, 1):
            halo_copy(0, side, c, y1).start()

    loads[1].wait()
    loads[2].wait()

    def element(degree, side, s, now, older, store):
        p = side * edge + s
        i = perm_ref[p]
        inner = now[pos_ref[lax.rem(neigh_ref[i, 1 - side], local)]]
        left = now[pos_ref[lax.rem(neigh_ref[i, 2], local)]]
        right = now[pos_ref[lax.rem(neigh_ref[i, 3], local)]]
        outer = halo[degree, side, s]
        mine = now[p]
        vertical = [inner, outer] if side else [outer, inner]
        stacked = jnp.concatenate([mine] + vertical + [left, right], axis=0)
        applied = jnp.dot(h[i], stacked, preferred_element_type=jnp.float32)
        following = (2.0 / spectral_half) * (
            applied - center_value * mine.astype(jnp.float32)
        ) - older(p, i).astype(jnp.float32)
        store[p] = jnp.where(row_index < size_ref[i], following, 0.0).astype(jnp.bfloat16)

    def first(c, _):
        halo_arrived(0, 0, c)
        halo_arrived(0, 1, c)
        for k in range(q):
            for side in (0, 1):
                element(0, side, c * q + k, y1, lambda p, i: prev[i], y2)
        for side in (0, 1):
            halo_copy(1, side, c, y2).start()
        return 0

    lax.fori_loop(0, CHUNKS, first, 0)

    gram[...] = jnp.zeros_like(gram)
    cross[...] = jnp.zeros_like(cross)

    def x_copy(j, c):
        to = lax.rem(b + j, count_band)
        start = jnp.where(to < b, 0, edge)
        return pltpu.make_async_remote_copy(
            src_ref=f.at[pl.ds(start + c * q, q)],
            dst_ref=other.at[count_band - j - 1, pl.ds(c * q, q)],
            send_sem=x_send.at[j - 1, c],
            recv_sem=x_recv.at[count_band - j - 1, c],
            device_id=(e, to),
            device_id_type=MESH,
        )

    def x_arrived(j, c):
        pltpu.make_async_remote_copy(
            src_ref=f.at[pl.ds(0, q)],
            dst_ref=other.at[j - 1, pl.ds(c * q, q)],
            send_sem=x_send.at[j - 1, c],
            recv_sem=x_recv.at[j - 1, c],
            device_id=(e, lax.rem(b + j, count_band)),
            device_id_type=MESH,
        ).wait_recv()

    def add_cross(c):
        for j in range(1, count_band):
            x_arrived(j, c)
            start = jnp.where(b < lax.rem(b + j, count_band), 0, edge)
            mine = f[pl.ds(start + c * q, q)].reshape(q * bmax, bands)
            theirs = other[j - 1, pl.ds(c * q, q)].reshape(q * bmax, bands)
            cross[j - 1] += lax.dot_general(mine, theirs, ROWS, preferred_element_type=jnp.float32)

    def second(c, _):
        halo_arrived(1, 0, c)
        halo_arrived(1, 1, c)
        for k in range(q):
            for side in (0, 1):
                element(1, side, c * q + k, y2, lambda p, i: y1[p], f)
        for j in range(1, count_band):
            x_copy(j, c).start()
        for side in (0, 1):
            block = f[pl.ds(side * edge + c * q, q)].reshape(q * bmax, bands)
            gram[...] += lax.dot_general(block, block, ROWS, preferred_element_type=jnp.float32)

        @pl.when(c > 0)
        def _():
            add_cross(c - 1)

        return 0

    lax.fori_loop(0, CHUNKS, second, 0)

    def give(i, _):
        ordered[i] = f[pos_ref[i]]
        return 0

    lax.fori_loop(0, local, give, 0, unroll=4)
    store = pltpu.make_async_copy(ordered, out_hbm, out_sem)
    store.start()

    def put_w(block, matrix):
        for k in range(per_block):
            w[k % 2, block * (per_block // 2) + k // 2] = matrix[k * rows:(k + 1) * rows].astype(jnp.bfloat16)

    put_w(b, gram[...])
    add_cross(CHUNKS - 1)
    for j in range(1, count_band):
        matrix = cross[j - 1]
        put_w(lax.rem(b + j, count_band), matrix.T)
        for k in range(per_block):
            v[k % 2, j - 1, k // 2] = matrix[k * rows:(k + 1) * rows].astype(jnp.bfloat16)

    def pair_copy(n, source, target):
        return pltpu.make_async_remote_copy(
            src_ref=source.at[1 - parity],
            dst_ref=target,
            send_sem=pair_send.at[n],
            recv_sem=pair_recv.at[n],
            device_id=(partner, b),
            device_id_type=MESH,
        )

    pairs = [pair_copy(0, w, w1), pair_copy(1, v, v1)]
    for copy in pairs:
        copy.start()
    pairs[0].wait_recv()
    w2[...] = (w[parity].astype(jnp.float32) + w1[...].astype(jnp.float32)).astype(jnp.bfloat16)
    pairs[1].wait_recv()
    v2[...] = (v[parity].astype(jnp.float32) + v1[...].astype(jnp.float32)).astype(jnp.bfloat16)

    def w_copy(d):
        to = lax.rem(pair + d, half)
        return pltpu.make_async_remote_copy(
            src_ref=w2.at[to],
            dst_ref=rw.at[half - d - 1],
            send_sem=w_send.at[d - 1],
            recv_sem=w_recv.at[half - d - 1],
            device_id=(2 * to + parity, b),
            device_id_type=MESH,
        )

    def v_copy(j, k):
        return pltpu.make_async_remote_copy(
            src_ref=v2.at[j - 1, k],
            dst_ref=rv.at[pair],
            send_sem=v_send.at[j - 1, k],
            recv_sem=v_recv.at[pair],
            device_id=(b * per_block + 2 * k + parity, lax.rem(b + j, count_band)),
            device_id_type=MESH,
        )

    sends = [w_copy(d) for d in range(1, half)]
    sends += [v_copy(j, k) for j in range(1, count_band) for k in range(per_block // 2)]
    for copy in sends:
        copy.start()

    margin_ref[...] = w2[pair].astype(jnp.float32)
    for d in range(1, half):
        pltpu.make_async_remote_copy(
            src_ref=w2.at[0],
            dst_ref=rw.at[d - 1],
            send_sem=w_send.at[d - 1],
            recv_sem=w_recv.at[d - 1],
            device_id=(2 * lax.rem(pair + d, half) + parity, b),
            device_id_type=MESH,
        ).wait_recv()
        margin_ref[...] += rw[d - 1].astype(jnp.float32)

    block = lax.div(e, per_block)

    @pl.when(block != b)
    def _():
        for k in range(half):
            pltpu.make_async_remote_copy(
                src_ref=v2.at[0, 0],
                dst_ref=rv.at[k],
                send_sem=v_send.at[0, 0],
                recv_sem=v_recv.at[k],
                device_id=(2 * k + parity, block),
                device_id_type=MESH,
            ).wait_recv()
            margin_ref[...] += rv[k].astype(jnp.float32)

    margin_ref[...] = margin_ref[...] / jnp.float32(local * count_elem * bmax)

    for copy in pairs + sends:
        copy.wait_send()

    def drain(c, _):
        for side in (0, 1):
            halo_copy(0, side, c, y1).wait_send()
            halo_copy(1, side, c, y2).wait_send()
        for j in range(1, count_band):
            x_copy(j, c).wait_send()
        return 0

    lax.fori_loop(0, CHUNKS, drain, 0)
    store.wait()


def edge_order(neighbours):
    local = neighbours.shape[0]
    owners = neighbours[:, 0] // local
    ids = jnp.arange(local, dtype=jnp.int32)
    above = neighbours[:, 0] % local
    key = jnp.where(owners != lax.axis_index("elem"), above, local + ids)
    pos = jnp.sum((key[None, :] < key[:, None]).astype(jnp.int32), axis=1)
    perm = jnp.sum(jnp.where(pos[None, :] == ids[:, None], ids[None, :], 0), axis=1)
    return pos, perm


def on_device(count_elem, count_band, y_current, y_previous, h_blocks, basis_sizes, neighbours):
    local, bmax, bands = y_current.shape
    rows = bands * count_band // count_elem
    per_block = bands // rows
    half = count_elem // 2
    pos, perm = edge_order(neighbours)
    smem = pl.BlockSpec(memory_space=pltpu.SMEM)
    anywhere = pl.BlockSpec(memory_space=pl.ANY)
    bf16, f32 = jnp.bfloat16, jnp.float32
    dma = pltpu.SemaphoreType.DMA
    whole = (local, bmax, bands)
    others = count_band - 1
    slot = (rows, bands)
    return tuple(pl.pallas_call(
        functools.partial(kernel, count_elem, count_band),
        out_shape=(
            jax.ShapeDtypeStruct(whole, bf16),
            jax.ShapeDtypeStruct((rows, bands), f32),
        ),
        in_specs=[smem] * 4 + [anywhere] * 3,
        out_specs=(anywhere, pl.BlockSpec(memory_space=pltpu.VMEM)),
        scratch_shapes=[
            pltpu.VMEM(whole, bf16),
            pltpu.VMEM(whole, bf16),
            pltpu.VMEM(h_blocks.shape, bf16),
            pltpu.VMEM(whole, bf16),
            pltpu.VMEM(whole, bf16),
            pltpu.VMEM(whole, bf16),
            pltpu.VMEM(whole, bf16),
            pltpu.VMEM((2, 2, local // 2, bmax, bands), bf16),
            pltpu.VMEM((others, local // 2, bmax, bands), bf16),
            pltpu.VMEM((bands, bands), f32),
            pltpu.VMEM((others, bands, bands), f32),
            pltpu.VMEM((2, half) + slot, bf16),
            pltpu.VMEM((2, others, per_block // 2) + slot, bf16),
            pltpu.VMEM((half,) + slot, bf16),
            pltpu.VMEM((others, per_block // 2) + slot, bf16),
            pltpu.VMEM((half,) + slot, bf16),
            pltpu.VMEM((others, per_block // 2) + slot, bf16),
            pltpu.VMEM((half - 1,) + slot, bf16),
            pltpu.VMEM((half,) + slot, bf16),
            dma((3,)),
            dma,
            dma((2, 2, CHUNKS)),
            dma((2, 2, CHUNKS)),
            dma((others, CHUNKS)),
            dma((others, CHUNKS)),
            dma((2,)),
            dma((2,)),
            dma((half - 1,)),
            dma((half - 1,)),
            dma((others, per_block // 2)),
            dma((half,)),
        ],
        compiler_params=pltpu.CompilerParams(
            collective_id=0, has_side_effects=True, vmem_limit_bytes=48 * 1024 * 1024
        ),
    )(pos, perm, neighbours, basis_sizes, y_current, y_previous, h_blocks))


def solution(mesh):
    in_specs = (
        P("elem", None, "band"),
        P("elem", None, "band"),
        P("elem", None, None),
        P("elem"),
        P("elem", None),
    )
    out_specs = (P("elem", None, "band"), P("elem", "band"))
    body = functools.partial(on_device, mesh.shape["elem"], mesh.shape["band"])
    return jax.shard_map(body, mesh=mesh, in_specs=in_specs, out_specs=out_specs, check_vma=False)
```

time: 175 us -> 56.8 us (0.32)
  the two profiles are of different devices: /device:TPU:0 before, /device:TPU:25 now
where the time goes in v1:
time: 56.8 us; the launch traced here: 56.5 us
  Pallas kernels  47.3 us (83%)
  local copies, waits for them, and re-layouts  6.87 us (12%)
  other arithmetic  1.68 us (3%)
  between operations  0.65 us (1%)
    pallas_call x1, Pallas kernels, on_device(): pl.pallas_call(functools.partial(kernel, count_elem, count_band), out_sha...  47.3 us
    unnamed x11, local copies, waits for them, and re-layouts  6.87 us

profile of v1, /device:TPU:25, one launch (start us, length us, event | category | flops | bytes accessed | tf_op | source)
XLA Modules:
  0.0 56.5 jit_solution(11146538283122414011)
XLA Ops:
  0.6 0.7 %fusion = s32[32]{0:T(128)S(1)} fusion(s32[32,4]{0,1:T(4,128)} %param.9, s32[]{:T(128)S(6)} %axis_index.15), kind=kLoop, calls=%fused_computation.16 | loop fusion | flops 704 | bytes 260 | tf_op jit(solution)/shard_map/lt | solution.py:290
  1.3 0.7 %compare_select_fusion.1 = s32[32]{0:T(128)S(1)} fusion(s32[32,4]{0,1:T(4,128)} %param.9, s32[]{:T(128)S(6)} %axis_index.15), kind=kLoop, calls=%fused_computation.7 | loop fusion | flops 704 | bytes 260 | tf_op jit(solution)/shard_map/jit(_where)/select_n | solution.py:289
  2.0 0.2 convert_reduce_fusion.pos_ref
  2.2 0.1 select_reduce_fusion.perm_ref
  2.3 0.8 %copy.8.neigh_ref = s32[32,4]{1,0:T(8,128)S(1)} copy(s32[32,4]{0,1:T(4,128)} %param.9) | data formatting | bytes 1024 | tf_op args[4]
  3.1 0.0 copy-start
  3.1 1.4 %copy-done = bf16[32,64,320]{2,1,0:T(8,128)(2,1)S(1)} copy-done((bf16[32,64,320]{2,1,0:T(8,128)(2,1)S(1)}, bf16[32,64,320]{2,1,0:T(8,128)(2,1)}, u32[]{:S(2)}) %copy-start) | copy-done | bytes 1310744
  4.5 0.0 copy-start.1
  4.5 1.2 %copy-done.1 = bf16[32,64,256]{2,1,0:T(8,128)(2,1)S(1)} copy-done((bf16[32,64,256]{2,1,0:T(8,128)(2,1)S(1)}, bf16[32,64,256]{2,1,0:T(8,128)(2,1)}, u32[]{:S(2)}) %copy-start.1) | copy-done | bytes 1048600
  5.7 0.0 copy-start.2
  5.7 1.2 %copy-done.2 = bf16[32,64,256]{2,1,0:T(8,128)(2,1)S(1)} copy-done((bf16[32,64,256]{2,1,0:T(8,128)(2,1)S(1)}, bf16[32,64,256]{2,1,0:T(8,128)(2,1)}, u32[]{:S(2)}) %copy-start.2) | copy-done | bytes 1048600
  6.9 0.0 copy-start.3
  6.9 0.7 %copy-done.3 = s32[32]{0:T(128)S(1)} copy-done((s32[32]{0:T(128)S(1)}, s32[32]{0:T(128)}, u32[]{:S(2)}) %copy-start.3) | copy-done | bytes 152
  7.6 47.3 %shard_map.68 = (bf16[32,64,256]{2,1,0:T(8,128)(2,1)S(1)}, f32[32,256]{1,0:T(8,128)S(1)}) custom-call(s32[32]{0:T(128)S(1)} %convert_reduce_fusion.pos_ref, s32[32]{0:T(128)S(1)} %select_reduce_fusion.perm_ref, s32[32,4]{1,0:T(8,128)S(1)} %copy.8.neigh_ref, s32[32]{0:T(128)S(1)} %copy-done.3, bf16[32,64,256]{2,1,0:T(8,128)(2,1)S(1)} %copy-done.1, ...), custom_call_target="tpu_custom_call" | custom-call | tf_op jit(solution)/shard_map/pallas_call | solution.py:308
  54.9 1.0 %copy.11 = bf16[32,64,256]{2,1,0:T(8,128)(2,1)} copy(bf16[32,64,256]{2,1,0:T(8,128)(2,1)S(1)} %get-tuple-element.4) | data formatting | bytes 2097152
  55.9 0.6 %copy.12 = f32[32,256]{1,0:T(8,128)} copy(f32[32,256]{1,0:T(8,128)S(1)} %get-tuple-element.5) | data formatting | bytes 65536
Async XLA Ops:
  3.1 1.4 %copy-start = (bf16[32,64,320]{2,1,0:T(8,128)(2,1)S(1)}, bf16[32,64,320]{2,1,0:T(8,128)(2,1)}, u32[]{:S(2)}) copy-start(bf16[32,64,320]{2,1,0:T(8,128)(2,1)} %h_hbm.1) | copy-start | bytes 3932164
  4.5 1.2 %copy-start.1 = (bf16[32,64,256]{2,1,0:T(8,128)(2,1)S(1)}, bf16[32,64,256]{2,1,0:T(8,128)(2,1)}, u32[]{:S(2)}) copy-start(bf16[32,64,256]{2,1,0:T(8,128)(2,1)} %cur_hbm.1) | copy-start | bytes 3145732
  5.7 1.2 %copy-start.2 = (bf16[32,64,256]{2,1,0:T(8,128)(2,1)S(1)}, bf16[32,64,256]{2,1,0:T(8,128)(2,1)}, u32[]{:S(2)}) copy-start(bf16[32,64,256]{2,1,0:T(8,128)(2,1)} %prev_hbm.1) | copy-start | bytes 3145732
  6.9 0.7 %copy-start.3 = (s32[32]{0:T(128)S(1)}, s32[32]{0:T(128)}, u32[]{:S(2)}) copy-start(s32[32]{0:T(128)} %size_ref.1) | copy-start | bytes 388

commit v2 on v1

v2 whole, which is shorter than its diff:
```python
import functools

import jax
import jax.numpy as jnp
from jax import lax
from jax.experimental import pallas as pl
from jax.experimental.pallas import tpu as pltpu
from jax.sharding import PartitionSpec as P

GROUP = 2
center_value = 0.3
spectral_half = 1.7
MESH = pl.DeviceIdType.MESH
ROWS = (((0,), (0,)), ((), ()))


def kernel(
    count_elem, count_band,
    neigh_hbm, size_hbm, cur_hbm, prev_hbm, h_hbm,
    out_hbm, margin_ref,
    neigh_vec, table_vec, neigh_ref, size_ref, table,
    cur, prev, h, y1, y2, f, ordered, halo, other, gram, cross,
    w, v, w1, v1, w2, v2, rw, rv,
    load_sem, out_sem, halo_send, halo_recv, x_send, x_recv,
    pair_send, pair_recv, w_send, w_recv, v_send, v_recv,
):
    e = lax.axis_index("elem")
    b = lax.axis_index("band")
    local, bmax, bands = y1.shape
    edge = local // 2
    q = GROUP
    chunks = edge // q
    half = count_elem // 2
    rows = margin_ref.shape[0]
    per_block = bands // rows
    parity = lax.rem(e, 2)
    pair = lax.div(e, 2)
    fast, slow = 1 - parity, parity
    partner = e + 1 - 2 * parity
    neighbour = lax.rem(e + count_elem - 1 + 2 * parity, count_elem)

    sources = (neigh_hbm, neigh_hbm, size_hbm, cur_hbm, prev_hbm, h_hbm)
    targets = (neigh_vec, neigh_ref, size_ref, cur, prev, h)
    loads = [
        pltpu.make_async_copy(source, target, load_sem.at[k])
        for k, (source, target) in enumerate(zip(sources, targets))
    ]
    for load in loads:
        load.start()

    barrier = pltpu.get_barrier_semaphore()
    for target in (neighbour, partner):
        pl.semaphore_signal(barrier, inc=1, device_id=(target, b), device_id_type=MESH)
    for j in range(count_band):
        for d in range(half):
            if j or d:
                target = (2 * lax.rem(pair + d, half) + parity, lax.rem(b + j, count_band))
                pl.semaphore_signal(barrier, inc=1, device_id=target, device_id_type=MESH)

    loads[0].wait()
    above = neigh_vec[0:1, :]
    lane = lax.broadcasted_iota(jnp.int32, (1, local), 1)
    key = jnp.where(lax.div(above, local) != e, lax.rem(above, local), local + lane)
    key = key * local + lane
    key_row = jnp.broadcast_to(key, (local, local))
    down = lax.broadcasted_iota(jnp.int32, (local, local), 0)
    across = lax.broadcasted_iota(jnp.int32, (local, local), 1)
    key_col = jnp.sum(jnp.where(down == across, key_row, 0), axis=1, keepdims=True)
    pos_row = jnp.sum(jnp.where(key_col < key_row, 1, 0), axis=0, keepdims=True)
    pos_col = jnp.sum(jnp.where(key_row < key_col, 1, 0), axis=1, keepdims=True)
    perm_row = jnp.sum(jnp.where(pos_col == across, down, 0), axis=0, keepdims=True)
    table_vec[0:1, 0:local] = pos_row
    table_vec[1:2, 0:local] = perm_row
    order = pltpu.make_async_copy(table_vec, table, load_sem.at[len(loads)])
    order.start()

    row_index = lax.broadcasted_iota(jnp.int32, (bmax, bands), 0)

    for load in loads[1:4]:
        load.wait()
    order.wait()

    def place(start):
        def one(k, _):
            p = start + k
            i = table[1, p]
            y1[p] = jnp.where(row_index < size_ref[i], cur[i].astype(jnp.float32), 0.0).astype(jnp.bfloat16)
            return 0

        lax.fori_loop(0, edge, one, 0, unroll=4)

    def slow_copy(degree, c, source):
        return pltpu.make_async_remote_copy(
            src_ref=source.at[pl.ds(slow * edge + c * q, q)],
            dst_ref=halo.at[degree, 0, pl.ds(c * q, q)],
            send_sem=halo_send.at[degree, c],
            recv_sem=halo_recv.at[degree, c],
            device_id=(neighbour, b),
            device_id_type=MESH,
        )

    def fast_copy(degree, source):
        return pltpu.make_async_remote_copy(
            src_ref=source.at[pl.ds(fast * edge, edge)],
            dst_ref=halo.at[degree, 1],
            send_sem=halo_send.at[degree, chunks],
            recv_sem=halo_recv.at[degree, chunks],
            device_id=(partner, b),
            device_id_type=MESH,
        )

    place(slow * edge)
    pl.semaphore_wait(barrier, 2 + half * count_band - 1)
    for c in range(chunks):
        slow_copy(0, c, y1).start()
    place(fast * edge)
    fast_copy(0, y1).start()

    loads[4].wait()
    loads[5].wait()

    def element(degree, side, s, now, older, store):
        p = side * edge + s
        i = table[1, p]
        inner = now[table[0, lax.rem(neigh_ref[1 - side, i], local)]]
        left = now[table[0, lax.rem(neigh_ref[2, i], local)]]
        right = now[table[0, lax.rem(neigh_ref[3, i], local)]]
        outer = halo[degree, jnp.where(side == fast, 1, 0), s]
        mine = now[p]
        upper = jnp.where(side == 0, outer, inner)
        lower = jnp.where(side == 0, inner, outer)
        stacked = jnp.concatenate([mine, upper, lower, left, right], axis=0)
        applied = jnp.dot(h[i], stacked, preferred_element_type=jnp.float32)
        following = (2.0 / spectral_half) * (
            applied - center_value * mine.astype(jnp.float32)
        ) - older(p, i).astype(jnp.float32)
        store[p] = jnp.where(row_index < size_ref[i], following, 0.0).astype(jnp.bfloat16)

    def older_first(p, i):
        return prev[i]

    def older_second(p, i):
        return y1[p]

    def first_fast(g, _):
        for k in range(4):
            element(0, fast, g * 4 + k, y1, older_first, y2)
        return 0

    fast_copy(0, y1).wait_recv()
    lax.fori_loop(0, edge // 4, first_fast, 0)
    fast_copy(1, y2).start()

    def first_slow(c, _):
        slow_copy(0, c, y1).wait_recv()
        for k in range(q):
            element(0, slow, c * q + k, y1, older_first, y2)
        slow_copy(1, c, y2).start()
        return 0

    lax.fori_loop(0, chunks, first_slow, 0)

    gram[...] = jnp.zeros_like(gram)
    cross[...] = jnp.zeros_like(cross)

    def sent_side(j):
        return jnp.where(lax.rem(b + j, count_band) < b, 0, 1)

    def x_copy(j, c):
        return pltpu.make_async_remote_copy(
            src_ref=f.at[pl.ds(sent_side(j) * edge + c * q, q)],
            dst_ref=other.at[count_band - j - 1, pl.ds(c * q, q)],
            send_sem=x_send.at[j - 1, c],
            recv_sem=x_recv.at[count_band - j - 1, c],
            device_id=(e, lax.rem(b + j, count_band)),
            device_id_type=MESH,
        )

    def x_start(side, c):
        for j in range(1, count_band):
            @pl.when(sent_side(j) == side)
            def _():
                x_copy(j, c).start()

    def x_arrived(j, c):
        pltpu.make_async_remote_copy(
            src_ref=f.at[pl.ds(0, q)],
            dst_ref=other.at[j - 1, pl.ds(c * q, q)],
            send_sem=x_send.at[j - 1, c],
            recv_sem=x_recv.at[j - 1, c],
            device_id=(e, lax.rem(b + j, count_band)),
            device_id_type=MESH,
        ).wait_recv()

    def add_gram(first, count):
        block = f[pl.ds(first, count)].reshape(count * bmax, bands)
        gram[...] += lax.dot_general(block, block, ROWS, preferred_element_type=jnp.float32)

    def add_cross(c):
        for j in range(1, count_band):
            x_arrived(j, c)
            start = (1 - sent_side(j)) * edge
            mine = f[pl.ds(start + c * q, q)].reshape(q * bmax, bands)
            theirs = other[j - 1, pl.ds(c * q, q)].reshape(q * bmax, bands)
            cross[j - 1] += lax.dot_general(mine, theirs, ROWS, preferred_element_type=jnp.float32)

    fast_copy(1, y2).wait_recv()

    def second_fast(g, _):
        for k in range(4):
            element(1, fast, g * 4 + k, y2, older_second, f)
        for k in range(4 // q):
            x_start(fast, g * (4 // q) + k)
        return 0

    lax.fori_loop(0, edge // 4, second_fast, 0)

    def gram_fast(g, _):
        add_gram(fast * edge + g * 4, 4)
        return 0

    lax.fori_loop(0, edge // 4, gram_fast, 0)

    def second_slow(c, _):
        slow_copy(1, c, y2).wait_recv()
        for k in range(q):
            element(1, slow, c * q + k, y2, older_second, f)
        x_start(slow, c)
        add_gram(slow * edge + c * q, q)

        @pl.when(c > 0)
        def _():
            add_cross(c - 1)

        return 0

    lax.fori_loop(0, chunks, second_slow, 0)

    def give(i, _):
        ordered[i] = f[table[0, i]]
        return 0

    lax.fori_loop(0, local, give, 0, unroll=4)
    store = pltpu.make_async_copy(ordered, out_hbm, out_sem)
    store.start()

    def put_w(block, matrix):
        for k in range(per_block):
            w[k % 2, block * (per_block // 2) + k // 2] = matrix[k * rows:(k + 1) * rows].astype(jnp.bfloat16)

    put_w(b, gram[...])
    add_cross(chunks - 1)
    for j in range(1, count_band):
        matrix = cross[j - 1]
        put_w(lax.rem(b + j, count_band), matrix.T)
        for k in range(per_block):
            v[k % 2, j - 1, k // 2] = matrix[k * rows:(k + 1) * rows].astype(jnp.bfloat16)

    def pair_copy(n, source, target):
        return pltpu.make_async_remote_copy(
            src_ref=source.at[1 - parity],
            dst_ref=target,
            send_sem=pair_send.at[n],
            recv_sem=pair_recv.at[n],
            device_id=(partner, b),
            device_id_type=MESH,
        )

    pairs = [pair_copy(0, w, w1), pair_copy(1, v, v1)]
    for copy in pairs:
        copy.start()
    pairs[0].wait_recv()
    w2[...] = (w[parity].astype(jnp.float32) + w1[...].astype(jnp.float32)).astype(jnp.bfloat16)
    pairs[1].wait_recv()
    v2[...] = (v[parity].astype(jnp.float32) + v1[...].astype(jnp.float32)).astype(jnp.bfloat16)

    def w_copy(d):
        to = lax.rem(pair + d, half)
        return pltpu.make_async_remote_copy(
            src_ref=w2.at[to],
            dst_ref=rw.at[half - d - 1],
            send_sem=w_send.at[d - 1],
            recv_sem=w_recv.at[half - d - 1],
            device_id=(2 * to + parity, b),
            device_id_type=MESH,
        )

    def v_copy(j, k):
        return pltpu.make_async_remote_copy(
            src_ref=v2.at[j - 1, k],
            dst_ref=rv.at[pair],
            send_sem=v_send.at[j - 1, k],
            recv_sem=v_recv.at[pair],
            device_id=(b * per_block + 2 * k + parity, lax.rem(b + j, count_band)),
            device_id_type=MESH,
        )

    sends = [w_copy(d) for d in range(1, half)]
    sends += [v_copy(j, k) for j in range(1, count_band) for k in range(per_block // 2)]
    for copy in sends:
        copy.start()

    margin_ref[...] = w2[pair].astype(jnp.float32)
    for d in range(1, half):
        pltpu.make_async_remote_copy(
            src_ref=w2.at[0],
            dst_ref=rw.at[d - 1],
            send_sem=w_send.at[d - 1],
            recv_sem=w_recv.at[d - 1],
            device_id=(2 * lax.rem(pair + d, half) + parity, b),
            device_id_type=MESH,
        ).wait_recv()
        margin_ref[...] += rw[d - 1].astype(jnp.float32)

    block = lax.div(e, per_block)

    @pl.when(block != b)
    def _():
        for k in range(half):
            pltpu.make_async_remote_copy(
                src_ref=v2.at[0, 0],
                dst_ref=rv.at[k],
                send_sem=v_send.at[0, 0],
                recv_sem=v_recv.at[k],
                device_id=(2 * k + parity, block),
                device_id_type=MESH,
            ).wait_recv()
            margin_ref[...] += rv[k].astype(jnp.float32)

    margin_ref[...] = margin_ref[...] / jnp.float32(local * count_elem * bmax)

    for copy in pairs + sends:
        copy.wait_send()

    fast_copy(0, y1).wait_send()
    fast_copy(1, y2).wait_send()

    def drain(c, _):
        slow_copy(0, c, y1).wait_send()
        slow_copy(1, c, y2).wait_send()
        for j in range(1, count_band):
            x_copy(j, c).wait_send()
        return 0

    lax.fori_loop(0, chunks, drain, 0)
    store.wait()


def on_device(count_elem, count_band, y_current, y_previous, h_blocks, basis_sizes, neighbours):
    local, bmax, bands = y_current.shape
    rows = bands * count_band // count_elem
    per_block = bands // rows
    half = count_elem // 2
    smem = pltpu.SMEM
    chunks = local // 2 // GROUP
    fixed = pl.BlockSpec(memory_space=pltpu.HBM)
    anywhere = pl.BlockSpec(memory_space=pl.ANY)
    bf16, f32 = jnp.bfloat16, jnp.float32
    dma = pltpu.SemaphoreType.DMA
    whole = (local, bmax, bands)
    others = count_band - 1
    slot = (rows, bands)
    return tuple(pl.pallas_call(
        functools.partial(kernel, count_elem, count_band),
        out_shape=(
            jax.ShapeDtypeStruct(whole, bf16),
            jax.ShapeDtypeStruct((rows, bands), f32),
        ),
        in_specs=[fixed] * 5,
        out_specs=(anywhere, pl.BlockSpec(memory_space=pltpu.VMEM)),
        scratch_shapes=[
            pltpu.VMEM((4, local), jnp.int32),
            pltpu.VMEM((8, 128), jnp.int32),
            smem((4, local), jnp.int32),
            smem((local,), jnp.int32),
            smem((8, 128), jnp.int32),
            pltpu.VMEM(whole, bf16),
            pltpu.VMEM(whole, bf16),
            pltpu.VMEM(h_blocks.shape, bf16),
            pltpu.VMEM(whole, bf16),
            pltpu.VMEM(whole, bf16),
            pltpu.VMEM(whole, bf16),
            pltpu.VMEM(whole, bf16),
            pltpu.VMEM((2, 2, local // 2, bmax, bands), bf16),
            pltpu.VMEM((others, local // 2, bmax, bands), bf16),
            pltpu.VMEM((bands, bands), f32),
            pltpu.VMEM((others, bands, bands), f32),
            pltpu.VMEM((2, half) + slot, bf16),
            pltpu.VMEM((2, others, per_block // 2) + slot, bf16),
            pltpu.VMEM((half,) + slot, bf16),
            pltpu.VMEM((others, per_block // 2) + slot, bf16),
            pltpu.VMEM((half,) + slot, bf16),
            pltpu.VMEM((others, per_block // 2) + slot, bf16),
            pltpu.VMEM((half - 1,) + slot, bf16),
            pltpu.VMEM((half,) + slot, bf16),
            dma((7,)),
            dma,
            dma((2, chunks + 1)),
            dma((2, chunks + 1)),
            dma((others, chunks)),
            dma((others, chunks)),
            dma((2,)),
            dma((2,)),
            dma((half - 1,)),
            dma((half - 1,)),
            dma((others, per_block // 2)),
            dma((half,)),
        ],
        compiler_params=pltpu.CompilerParams(
            collective_id=0, has_side_effects=True, vmem_limit_bytes=67_000_000
        ),
    )(neighbours.T, basis_sizes, y_current, y_previous, h_blocks))


def solution(mesh):
    in_specs = (
        P("elem", None, "band"),
        P("elem", None, "band"),
        P("elem", None, None),
        P("elem"),
        P("elem", None),
    )
    out_specs = (P("elem", None, "band"), P("elem", "band"))
    body = functools.partial(on_device, mesh.shape["elem"], mesh.shape["band"])
    return jax.shard_map(body, mesh=mesh, in_specs=in_specs, out_specs=out_specs, check_vma=False)
```

time: 56.8 us -> 47.8 us (0.84)
  the two profiles are of different devices: /device:TPU:25 before, /device:TPU:3 now
where the time goes in v2:
time: 47.8 us; the launch traced here: 47.6 us
  Pallas kernels  44.1 us (92%)
  local copies, waits for them, and re-layouts  2.93 us (6%)
  between operations  0.65 us (1%)
    pallas_call x1, Pallas kernels, on_device(): pl.pallas_call(functools.partial(kernel, count_elem, count_band), out_sha...  44.1 us
    unnamed x4, local copies, waits for them, and re-layouts  2.93 us

profile of v2, /device:TPU:3, one launch (start us, length us, event | category | flops | bytes accessed | tf_op | source)
XLA Modules:
  0.0 47.6 jit_solution(14112935615064617475)
XLA Ops:
  0.6 44.1 %shard_map.68 = (bf16[32,64,256]{2,1,0:T(8,128)(2,1)}, f32[32,256]{1,0:T(8,128)}) custom-call(s32[4,32]{1,0:T(4,128)} %bitcast.1, s32[32]{0:T(128)} %size_hbm.1, bf16[32,64,256]{2,1,0:T(8,128)(2,1)} %cur_hbm.1, bf16[32,64,256]{2,1,0:T(8,128)(2,1)} %prev_hbm.1, bf16[32,64,320]{2,1,0:T(8,128)(2,1)} %h_hbm.1), custom_call_target="tpu_custom_call" | custom-call | tf_op jit(solution)/shard_map/pallas_call | solution.py:363
  44.7 0.0 copy-start
  44.7 2.3 %copy.9 = bf16[32,64,256]{2,1,0:T(8,128)(2,1)} copy(bf16[32,64,256]{2,1,0:T(8,128)(2,1)} %get-tuple-element.4) | data formatting | bytes 2097152
  47.0 0.0 copy-done
  47.0 0.6 %copy.10 = f32[32,256]{1,0:T(8,128)} copy(f32[32,256]{1,0:T(8,128)S(1)} %copy-done) | data formatting | bytes 65536
Async XLA Ops:
  44.7 2.3 %copy-start = (f32[32,256]{1,0:T(8,128)S(1)}, f32[32,256]{1,0:T(8,128)}, u32[]{:S(2)}) copy-start(f32[32,256]{1,0:T(8,128)} %get-tuple-element.5) | copy-start | bytes 98308

commit v3 on v2

--- a/solution.py
+++ b/solution.py
@@ -17,12 +17,12 @@
 def kernel(
     count_elem, count_band,
     neigh_hbm, size_hbm, cur_hbm, prev_hbm, h_hbm,
-    out_hbm, margin_ref,
+    out_ref, margin_ref,
     neigh_vec, table_vec, neigh_ref, size_ref, table,
-    cur, prev, h, y1, y2, f, ordered, halo, other, gram, cross,
-    w, v, w1, v1, w2, v2, rw, rv,
-    load_sem, out_sem, halo_send, halo_recv, x_send, x_recv,
-    pair_send, pair_recv, w_send, w_recv, v_send, v_recv,
+    cur, prev, h, y1, y2, f, halo, other, gram, cross,
+    w, w1, w2, rw, rv,
+    load_sem, halo_send, halo_recv, x_send, x_recv,
+    pair_send, pair_recv, w_send, w_recv, v_send, v_recv, far,
 ):
     e = lax.axis_index("elem")
     b = lax.axis_index("band")
@@ -51,11 +51,28 @@
     barrier = pltpu.get_barrier_semaphore()
     for target in (neighbour, partner):
         pl.semaphore_signal(barrier, inc=1, device_id=(target, b), device_id_type=MESH)
-    for j in range(count_band):
-        for d in range(half):
-            if j or d:
-                target = (2 * lax.rem(pair + d, half) + parity, lax.rem(b + j, count_band))
-                pl.semaphore_signal(barrier, inc=1, device_id=target, device_id_type=MESH)
+    for j in range(1, count_band):
+        pl.semaphore_signal(
+            barrier, inc=1, device_id=(e, lax.rem(b + j, count_band)), device_id_type=MESH
+        )
+
+    reach = [1]
+    while 2 * reach[-1] < half:
+        reach.append(2 * reach[-1])
+
+    def advance(step):
+        if 0 < step <= len(reach):
+            pl.semaphore_wait(far.at[step - 1], 2)
+        elif step == len(reach) + 1:
+            pl.semaphore_wait(far.at[step - 1], count_band - 1)
+        if step < len(reach):
+            for distance in (reach[step], count_elem - reach[step]):
+                target = (lax.rem(e + distance, count_elem), b)
+                pl.semaphore_signal(far.at[step], inc=1, device_id=target, device_id_type=MESH)
+        elif step == len(reach):
+            for j in range(1, count_band):
+                target = (e, lax.rem(b + j, count_band))
+                pl.semaphore_signal(far.at[step], inc=1, device_id=target, device_id_type=MESH)
 
     loads[0].wait()
     above = neigh_vec[0:1, :]
@@ -110,11 +127,12 @@
         )
 
     place(slow * edge)
-    pl.semaphore_wait(barrier, 2 + half * count_band - 1)
+    pl.semaphore_wait(barrier, 1 + count_band)
     for c in range(chunks):
         slow_copy(0, c, y1).start()
     place(fast * edge)
     fast_copy(0, y1).start()
+    advance(0)
 
     loads[4].wait()
     loads[5].wait()
@@ -150,6 +168,7 @@
     fast_copy(0, y1).wait_recv()
     lax.fori_loop(0, edge // 4, first_fast, 0)
     fast_copy(1, y2).start()
+    advance(1)
 
     def first_slow(c, _):
         slow_copy(0, c, y1).wait_recv()
@@ -159,6 +178,7 @@
         return 0
 
     lax.fori_loop(0, chunks, first_slow, 0)
+    advance(2)
 
     gram[...] = jnp.zeros_like(gram)
     cross[...] = jnp.zeros_like(cross)
@@ -214,6 +234,7 @@
         return 0
 
     lax.fori_loop(0, edge // 4, second_fast, 0)
+    advance(3)
 
     def gram_fast(g, _):
         add_gram(fast * edge + g * 4, 4)
@@ -236,58 +257,39 @@
 
     lax.fori_loop(0, chunks, second_slow, 0)
 
-    def give(i, _):
-        ordered[i] = f[table[0, i]]
-        return 0
-
-    lax.fori_loop(0, local, give, 0, unroll=4)
-    store = pltpu.make_async_copy(ordered, out_hbm, out_sem)
-    store.start()
-
-    def put_w(block, matrix):
+    def cut(target, matrix):
         for k in range(per_block):
-            w[k % 2, block * (per_block // 2) + k // 2] = matrix[k * rows:(k + 1) * rows].astype(jnp.bfloat16)
-
-    put_w(b, gram[...])
-    add_cross(chunks - 1)
-    for j in range(1, count_band):
-        matrix = cross[j - 1]
-        put_w(lax.rem(b + j, count_band), matrix.T)
-        for k in range(per_block):
-            v[k % 2, j - 1, k // 2] = matrix[k * rows:(k + 1) * rows].astype(jnp.bfloat16)
-
-    def pair_copy(n, source, target):
+            w[k % 2, target, k // 2] = matrix[k * rows:(k + 1) * rows].astype(jnp.bfloat16)
+
+    def pair_copy(n, first, count):
         return pltpu.make_async_remote_copy(
-            src_ref=source.at[1 - parity],
-            dst_ref=target,
+            src_ref=w.at[1 - parity, pl.ds(first, count)],
+            dst_ref=w1.at[pl.ds(first, count)],
             send_sem=pair_send.at[n],
             recv_sem=pair_recv.at[n],
             device_id=(partner, b),
             device_id_type=MESH,
         )
 
-    pairs = [pair_copy(0, w, w1), pair_copy(1, v, v1)]
-    for copy in pairs:
-        copy.start()
-    pairs[0].wait_recv()
-    w2[...] = (w[parity].astype(jnp.float32) + w1[...].astype(jnp.float32)).astype(jnp.bfloat16)
-    pairs[1].wait_recv()
-    v2[...] = (v[parity].astype(jnp.float32) + v1[...].astype(jnp.float32)).astype(jnp.bfloat16)
-
-    def w_copy(d):
-        to = lax.rem(pair + d, half)
-        return pltpu.make_async_remote_copy(
-            src_ref=w2.at[to],
-            dst_ref=rw.at[half - d - 1],
-            send_sem=w_send.at[d - 1],
-            recv_sem=w_recv.at[half - d - 1],
+    def pair_sum(n):
+        w2[n] = (w[parity, n].astype(jnp.float32) + w1[n].astype(jnp.float32)).astype(jnp.bfloat16)
+
+    others = count_band - 1
+
+    def w_copy(j, k):
+        to = lax.rem(b + j, count_band) * (per_block // 2) + k
+        return to, pltpu.make_async_remote_copy(
+            src_ref=w2.at[j, k],
+            dst_ref=rw.at[pair],
+            send_sem=w_send.at[j, k],
+            recv_sem=w_recv.at[pair],
             device_id=(2 * to + parity, b),
             device_id_type=MESH,
         )
 
     def v_copy(j, k):
         return pltpu.make_async_remote_copy(
-            src_ref=v2.at[j - 1, k],
+            src_ref=w2.at[others + j, k],
             dst_ref=rv.at[pair],
             send_sem=v_send.at[j - 1, k],
             recv_sem=v_recv.at[pair],
@@ -295,30 +297,70 @@
             device_id_type=MESH,
         )
 
-    sends = [w_copy(d) for d in range(1, half)]
-    sends += [v_copy(j, k) for j in range(1, count_band) for k in range(per_block // 2)]
-    for copy in sends:
+    def each_w(blocks, act):
+        for j in blocks:
+            for k in range(per_block // 2):
+                to, copy = w_copy(j, k)
+
+                @pl.when(to != pair)
+                def _():
+                    act(copy)
+
+    def start(copy):
         copy.start()
 
-    margin_ref[...] = w2[pair].astype(jnp.float32)
+    def sent(copy):
+        copy.wait_send()
+
+    cut(0, gram[...])
+    pairs = [pair_copy(0, 0, 1), pair_copy(1, 1, 2 * others)]
+    pairs[0].start()
+
+    for step in range(4, len(reach) + 2):
+        advance(step)
+
+    def give(i, _):
+        out_ref[i] = f[table[0, i]]
+        return 0
+
+    lax.fori_loop(0, local // 2, give, 0, unroll=4)
+    pairs[0].wait_recv()
+    pair_sum(0)
+    each_w([0], start)
+
+    add_cross(chunks - 1)
+    for j in range(1, count_band):
+        cut(others + j, cross[j - 1])
+        cut(j, cross[j - 1].T)
+    pairs[1].start()
+    lax.fori_loop(local // 2, local, give, 0, unroll=4)
+    pairs[1].wait_recv()
+    for n in range(1, 1 + 2 * others):
+        pair_sum(n)
+    cross_sends = [v_copy(j, k) for j in range(1, count_band) for k in range(per_block // 2)]
+    for copy in cross_sends:
+        copy.start()
+    each_w(range(1, count_band), start)
+
+    block = lax.div(e, per_block)
+    margin_ref[...] = w2[lax.rem(block - b + count_band, count_band), pair - block * (per_block // 2)].astype(jnp.float32)
     for d in range(1, half):
+        source = lax.rem(pair + d, half)
         pltpu.make_async_remote_copy(
-            src_ref=w2.at[0],
-            dst_ref=rw.at[d - 1],
-            send_sem=w_send.at[d - 1],
-            recv_sem=w_recv.at[d - 1],
-            device_id=(2 * lax.rem(pair + d, half) + parity, b),
+            src_ref=w2.at[0, 0],
+            dst_ref=rw.at[source],
+            send_sem=w_send.at[0, 0],
+            recv_sem=w_recv.at[source],
+            device_id=(2 * source + parity, b),
             device_id_type=MESH,
         ).wait_recv()
-        margin_ref[...] += rw[d - 1].astype(jnp.float32)
-
-    block = lax.div(e, per_block)
+        margin_ref[...] += rw[source].astype(jnp.float32)
 
     @pl.when(block != b)
     def _():
         for k in range(half):
             pltpu.make_async_remote_copy(
-                src_ref=v2.at[0, 0],
+                src_ref=w2.at[0, 0],
                 dst_ref=rv.at[k],
                 send_sem=v_send.at[0, 0],
                 recv_sem=v_recv.at[k],
@@ -329,8 +371,9 @@
 
     margin_ref[...] = margin_ref[...] / jnp.float32(local * count_elem * bmax)
 
-    for copy in pairs + sends:
+    for copy in pairs + cross_sends:
         copy.wait_send()
+    each_w(range(count_band), sent)
 
     fast_copy(0, y1).wait_send()
     fast_copy(1, y2).wait_send()
@@ -343,7 +386,6 @@
         return 0
 
     lax.fori_loop(0, chunks, drain, 0)
-    store.wait()
 
 
 def on_device(count_elem, count_band, y_current, y_previous, h_blocks, basis_sizes, neighbours):
@@ -354,7 +396,6 @@
     smem = pltpu.SMEM
     chunks = local // 2 // GROUP
     fixed = pl.BlockSpec(memory_space=pltpu.HBM)
-    anywhere = pl.BlockSpec(memory_space=pl.ANY)
     bf16, f32 = jnp.bfloat16, jnp.float32
     dma = pltpu.SemaphoreType.DMA
     whole = (local, bmax, bands)
@@ -367,7 +408,7 @@
             jax.ShapeDtypeStruct((rows, bands), f32),
         ),
         in_specs=[fixed] * 5,
-        out_specs=(anywhere, pl.BlockSpec(memory_space=pltpu.VMEM)),
+        out_specs=[pl.BlockSpec(memory_space=pltpu.VMEM)] * 2,
         scratch_shapes=[
             pltpu.VMEM((4, local), jnp.int32),
             pltpu.VMEM((8, 128), jnp.int32),
@@ -380,36 +421,35 @@
             pltpu.VMEM(whole, bf16),
             pltpu.VMEM(whole, bf16),
             pltpu.VMEM(whole, bf16),
-            pltpu.VMEM(whole, bf16),
             pltpu.VMEM((2, 2, local // 2, bmax, bands), bf16),
             pltpu.VMEM((others, local // 2, bmax, bands), bf16),
             pltpu.VMEM((bands, bands), f32),
             pltpu.VMEM((others, bands, bands), f32),
-            pltpu.VMEM((2, half) + slot, bf16),
-            pltpu.VMEM((2, others, per_block // 2) + slot, bf16),
+            pltpu.VMEM((2, 1 + 2 * others, per_block // 2) + slot, bf16),
+            pltpu.VMEM((1 + 2 * others, per_block // 2) + slot, bf16),
+            pltpu.VMEM((1 + 2 * others, per_block // 2) + slot, bf16),
             pltpu.VMEM((half,) + slot, bf16),
-            pltpu.VMEM((others, per_block // 2) + slot, bf16),
-            pltpu.VMEM((half,) + slot, bf16),
-            pltpu.VMEM((others, per_block // 2) + slot, bf16),
-            pltpu.VMEM((half - 1,) + slot, bf16),
             pltpu.VMEM((half,) + slot, bf16),
             dma((7,)),
-            dma,
             dma((2, chunks + 1)),
             dma((2, chunks + 1)),
             dma((others, chunks)),
             dma((others, chunks)),
             dma((2,)),
             dma((2,)),
-            dma((half - 1,)),
-            dma((half - 1,)),
+            dma((count_band, per_block // 2)),
+            dma((half,)),
             dma((others, per_block // 2)),
             dma((half,)),
+            pltpu.SemaphoreType.REGULAR((count_elem.bit_length() + 1,)),
         ],
         compiler_params=pltpu.CompilerParams(
-            collective_id=0, has_side_effects=True, vmem_limit_bytes=67_000_000
+            collective_id=0, has_side_effects=True, vmem_limit_bytes=48 * 1024 * 1024
         ),
-    )(neighbours.T, basis_sizes, y_current, y_previous, h_blocks))
+    )(*(
+        pltpu.with_memory_space_constraint(array, pltpu.HBM)
+        for array in (neighbours.T, basis_sizes, y_current, y_previous, h_blocks)
+    )))
 
 
 def solution(mesh):

time: 47.8 us -> 44.6 us (0.933)
  Pallas kernels: 44.1 us -> 42.2 us
  local copies, waits for them, and re-layouts: 2.93 us -> 1.59 us
    pallas_call x1, Pallas kernels: 44.1 us -> 42.2 us  [on_device(): pl.pallas_call(functools.partial(kernel, count_elem, count_band), out_sha...]
    unnamed x4 -> x2, local copies, waits for them, and re-layouts: 2.93 us -> 1.59 us
where the time goes in v3:
time: 44.6 us; the launch traced here: 44.4 us
  Pallas kernels  42.2 us (95%)
  local copies, waits for them, and re-layouts  1.59 us (4%)
  between operations  0.64 us (1%)
    pallas_call x1, Pallas kernels, on_device(): pl.pallas_call(functools.partial(kernel, count_elem, count_band), out_sha...  42.2 us
    unnamed x2, local copies, waits for them, and re-layouts  1.59 us

profile of v3, /device:TPU:3, one launch (start us, length us, event | category | flops | bytes accessed | tf_op | source)
XLA Modules:
  0.0 44.4 jit_solution(12430746518744241621)
XLA Ops:
  0.6 42.2 %shard_map.68 = (bf16[32,64,256]{2,1,0:T(8,128)(2,1)S(1)}, f32[32,256]{1,0:T(8,128)S(1)}) custom-call(s32[4,32]{1,0:T(4,128)} %bitcast.1, s32[32]{0:T(128)} %size_hbm.1, bf16[32,64,256]{2,1,0:T(8,128)(2,1)} %cur_hbm.1, bf16[32,64,256]{2,1,0:T(8,128)(2,1)} %prev_hbm.1, bf16[32,64,320]{2,1,0:T(8,128)(2,1)} %h_hbm.1), custom_call_target="tpu_custom_call" | custom-call | tf_op jit(solution)/shard_map/pallas_call | solution.py:404
  42.8 1.0 %copy.9 = bf16[32,64,256]{2,1,0:T(8,128)(2,1)} copy(bf16[32,64,256]{2,1,0:T(8,128)(2,1)S(1)} %get-tuple-element.4) | data formatting | bytes 2097152
  43.8 0.6 %copy.10 = f32[32,256]{1,0:T(8,128)} copy(f32[32,256]{1,0:T(8,128)S(1)} %get-tuple-element.5) | data formatting | bytes 65536

commit v4 on v3

--- a/solution.py
+++ b/solution.py
@@ -7,7 +7,7 @@
 from jax.experimental.pallas import tpu as pltpu
 from jax.sharding import PartitionSpec as P
 
-GROUP = 2
+GROUP = 4
 center_value = 0.3
 spectral_half = 1.7
 MESH = pl.DeviceIdType.MESH
@@ -45,7 +45,7 @@
         pltpu.make_async_copy(source, target, load_sem.at[k])
         for k, (source, target) in enumerate(zip(sources, targets))
     ]
-    for load in loads:
+    for load in loads[:4]:
         load.start()
 
     barrier = pltpu.get_barrier_semaphore()
@@ -95,6 +95,8 @@
 
     for load in loads[1:4]:
         load.wait()
+    for load in loads[4:]:
+        load.start()
     order.wait()
 
     def place(start):
@@ -276,6 +278,9 @@
 
     others = count_band - 1
 
+    def far_first(k):
+        return jnp.where(e < half, per_block // 2 - 1 - k, k)
+
     def w_copy(j, k):
         to = lax.rem(b + j, count_band) * (per_block // 2) + k
         return to, pltpu.make_async_remote_copy(
@@ -300,7 +305,7 @@
     def each_w(blocks, act):
         for j in blocks:
             for k in range(per_block // 2):
-                to, copy = w_copy(j, k)
+                to, copy = w_copy(j, far_first(k))
 
                 @pl.when(to != pair)
                 def _():
@@ -313,7 +318,7 @@
         copy.wait_send()
 
     cut(0, gram[...])
-    pairs = [pair_copy(0, 0, 1), pair_copy(1, 1, 2 * others)]
+    pairs = [pair_copy(0, 0, 1), pair_copy(1, 1 + others, others), pair_copy(2, 1, others)]
     pairs[0].start()
 
     for step in range(4, len(reach) + 2):
@@ -323,7 +328,7 @@
         out_ref[i] = f[table[0, i]]
         return 0
 
-    lax.fori_loop(0, local // 2, give, 0, unroll=4)
+    lax.fori_loop(0, local, give, 0, unroll=4)
     pairs[0].wait_recv()
     pair_sum(0)
     each_w([0], start)
@@ -331,15 +336,19 @@
     add_cross(chunks - 1)
     for j in range(1, count_band):
         cut(others + j, cross[j - 1])
+    pairs[1].start()
+    for j in range(1, count_band):
         cut(j, cross[j - 1].T)
-    pairs[1].start()
-    lax.fori_loop(local // 2, local, give, 0, unroll=4)
+    pairs[2].start()
     pairs[1].wait_recv()
-    for n in range(1, 1 + 2 * others):
-        pair_sum(n)
-    cross_sends = [v_copy(j, k) for j in range(1, count_band) for k in range(per_block // 2)]
+    for j in range(1, count_band):
+        pair_sum(others + j)
+    cross_sends = [v_copy(j, far_first(k)) for j in range(1, count_band) for k in range(per_block // 2)]
     for copy in cross_sends:
         copy.start()
+    pairs[2].wait_recv()
+    for j in range(1, count_band):
+        pair_sum(j)
     each_w(range(1, count_band), start)
 
     block = lax.div(e, per_block)
@@ -386,6 +395,17 @@
         return 0
 
     lax.fori_loop(0, chunks, drain, 0)
+
+
+def write_out(filtered, margin, filtered_out, margin_out, sem):
+    copies = [
+        pltpu.make_async_copy(filtered, filtered_out, sem.at[0]),
+        pltpu.make_async_copy(margin, margin_out, sem.at[1]),
+    ]
+    for copy in copies:
+        copy.start()
+    for copy in copies:
+        copy.wait()
 
 
 def on_device(count_elem, count_band, y_current, y_previous, h_blocks, basis_sizes, neighbours):
@@ -401,7 +421,7 @@
     whole = (local, bmax, bands)
     others = count_band - 1
     slot = (rows, bands)
-    return tuple(pl.pallas_call(
+    results = pl.pallas_call(
         functools.partial(kernel, count_elem, count_band),
         out_shape=(
             jax.ShapeDtypeStruct(whole, bf16),
@@ -435,8 +455,8 @@
             dma((2, chunks + 1)),
             dma((others, chunks)),
             dma((others, chunks)),
-            dma((2,)),
-            dma((2,)),
+            dma((3,)),
+            dma((3,)),
             dma((count_band, per_block // 2)),
             dma((half,)),
             dma((others, per_block // 2)),
@@ -449,7 +469,15 @@
     )(*(
         pltpu.with_memory_space_constraint(array, pltpu.HBM)
         for array in (neighbours.T, basis_sizes, y_current, y_previous, h_blocks)
-    )))
+    ))
+    anywhere = pl.BlockSpec(memory_space=pl.ANY)
+    return tuple(pl.pallas_call(
+        write_out,
+        out_shape=[jax.ShapeDtypeStruct(array.shape, array.dtype) for array in results],
+        in_specs=[pl.BlockSpec(memory_space=pltpu.VMEM)] * 2,
+        out_specs=[anywhere] * 2,
+        scratch_shapes=[dma((2,))],
+    )(*(pltpu.with_memory_space_constraint(array, pltpu.VMEM) for array in results)))
 
 
 def solution(mesh):

time: 44.6 us -> 43.2 us (0.969)
  local copies, waits for them, and re-layouts: 1.59 us -> 0 us
    unnamed x2 -> x0, local copies, waits for them, and re-layouts: 1.59 us -> none
    pallas_call x0 -> x1, Pallas kernels: none -> 0.99 us  [on_device(): pl.pallas_call(write_out, out_shape=[jax.ShapeDtypeStruct(array.shape, ar...]
    pallas_call x1, Pallas kernels: 42.2 us -> 41.4 us  [on_device(): pl.pallas_call(functools.partial(kernel, count_elem, count_band), out_sha...]
where the time goes in v4:
time: 43.2 us; the launch traced here: 43 us
  Pallas kernels  42.4 us (98%)
  between operations  0.64 us (1%)
    pallas_call x1, Pallas kernels, on_device(): pl.pallas_call(functools.partial(kernel, count_elem, count_band), out_sha...  41.4 us
    pallas_call x1, Pallas kernels, on_device(): pl.pallas_call(write_out, out_shape=[jax.ShapeDtypeStruct(array.shape, ar...  0.99 us

profile of v4, /device:TPU:3, one launch (start us, length us, event | category | flops | bytes accessed | tf_op | source)
XLA Modules:
  0.0 43.0 jit_solution(8369447563024834361)
XLA Ops:
  0.6 41.4 %shard_map.68 = (bf16[32,64,256]{2,1,0:T(8,128)(2,1)S(1)}, f32[32,256]{1,0:T(8,128)S(1)}) custom-call(s32[4,32]{1,0:T(4,128)} %bitcast.1, s32[32]{0:T(128)} %size_hbm.1, bf16[32,64,256]{2,1,0:T(8,128)(2,1)} %cur_hbm.1, bf16[32,64,256]{2,1,0:T(8,128)(2,1)} %prev_hbm.1, bf16[32,64,320]{2,1,0:T(8,128)(2,1)} %h_hbm.1), custom_call_target="tpu_custom_call" | custom-call | tf_op jit(solution)/shard_map/pallas_call | solution.py:424
  42.0 1.0 %shard_map.69 = (bf16[32,64,256]{2,1,0:T(8,128)(2,1)}, f32[32,256]{1,0:T(8,128)}) custom-call(bf16[32,64,256]{2,1,0:T(8,128)(2,1)S(1)} %get-tuple-element.4.filtered, f32[32,256]{1,0:T(8,128)S(1)} %get-tuple-element.5.margin), custom_call_target="tpu_custom_call" | custom-call | tf_op jit(solution)/shard_map/pallas_call | solution.py:474

commit v5 on v4

--- a/solution.py
+++ b/solution.py
@@ -7,7 +7,7 @@
 from jax.experimental.pallas import tpu as pltpu
 from jax.sharding import PartitionSpec as P
 
-GROUP = 4
+GROUP = 8
 center_value = 0.3
 spectral_half = 1.7
 MESH = pl.DeviceIdType.MESH
@@ -229,13 +229,12 @@
     fast_copy(1, y2).wait_recv()
 
     def second_fast(g, _):
-        for k in range(4):
-            element(1, fast, g * 4 + k, y2, older_second, f)
-        for k in range(4 // q):
-            x_start(fast, g * (4 // q) + k)
-        return 0
-
-    lax.fori_loop(0, edge // 4, second_fast, 0)
+        for k in range(q):
+            element(1, fast, g * q + k, y2, older_second, f)
+        x_start(fast, g)
+        return 0
+
+    lax.fori_loop(0, chunks, second_fast, 0)
     advance(3)
 
     def gram_fast(g, _):

time: 43.2 us -> 41.7 us (0.965)
  Pallas kernels: 42.4 us -> 40.9 us
    pallas_call x1, Pallas kernels: 41.4 us -> 39.9 us  [on_device(): pl.pallas_call(functools.partial(kernel, count_elem, count_band), out_sha...]
where the time goes in v5:
time: 41.7 us; the launch traced here: 41.5 us
  Pallas kernels  40.9 us (98%)
  between operations  0.64 us (2%)
    pallas_call x1, Pallas kernels, on_device(): pl.pallas_call(functools.partial(kernel, count_elem, count_band), out_sha...  39.9 us
    pallas_call x1, Pallas kernels, on_device(): pl.pallas_call(write_out, out_shape=[jax.ShapeDtypeStruct(array.shape, ar...  0.99 us

profile of v5, /device:TPU:3, one launch (start us, length us, event | category | flops | bytes accessed | tf_op | source)
XLA Modules:
  0.0 41.5 jit_solution(6563852598363618733)
XLA Ops:
  0.6 39.9 %shard_map.68 = (bf16[32,64,256]{2,1,0:T(8,128)(2,1)S(1)}, f32[32,256]{1,0:T(8,128)S(1)}) custom-call(s32[4,32]{1,0:T(4,128)} %bitcast.1, s32[32]{0:T(128)} %size_hbm.1, bf16[32,64,256]{2,1,0:T(8,128)(2,1)} %cur_hbm.1, bf16[32,64,256]{2,1,0:T(8,128)(2,1)} %prev_hbm.1, bf16[32,64,320]{2,1,0:T(8,128)(2,1)} %h_hbm.1), custom_call_target="tpu_custom_call" | custom-call | tf_op jit(solution)/shard_map/pallas_call | solution.py:423
  40.6 1.0 %shard_map.69 = (bf16[32,64,256]{2,1,0:T(8,128)(2,1)}, f32[32,256]{1,0:T(8,128)}) custom-call(bf16[32,64,256]{2,1,0:T(8,128)(2,1)S(1)} %get-tuple-element.4.filtered, f32[32,256]{1,0:T(8,128)S(1)} %get-tuple-element.5.margin), custom_call_target="tpu_custom_call" | custom-call | tf_op jit(solution)/shard_map/pallas_call | solution.py:473
